TPU v7x, 32 devices: a whole 2x2x4 slice. The times are simulated.
32 devices in a mesh: obs: 8 (over z, x), bel: 4 (over y, core).
Axes of the slice: x: 2, y: 2, z: 4, core: 2. Of those that a mesh axis runs over, the one named last changes fastest.
Arguments:
- alpha_set: bfloat16 [2048, 2048], P('bel'), may hold values from -600 to 600
- transitions: bfloat16 [16, 2048, 2048], P(None, 'obs'), may hold values from 0.0009994507 to 1
- obs_weights: float32 [256, 16, 2048], P('obs'), may hold values from 0.01 to 1
- rewards: float32 [16, 2048], replicated, may hold values from -1 to 1
- chosen_idx: int32 [1536, 16, 256], P('bel', None, 'obs'), may hold values from 0 to 2047
- chosen_action: int32 [1536], P('bel'), may hold values from 0 to 15
Outputs:
- new_alpha: float32 [1536, 2048], P(('bel', 'obs'))
Inputs may be any that keep to these rules, and one draw needn't show every extreme that they name: `chosen_idx`: an index into the 2048 alpha vectors. `chosen_action`: an index into the 16 actions.
All inputs are finite; a program needn't handle non-finite values.
Results may differ from a plain program's by a relative error of at most 0.0003.
Values may be sent and summed in bfloat16 or wider, within the bound.
A program may use at most 192 MiB of HBM per device.

v0:
```python
import jax
import jax.numpy as jnp
from jax import lax
from jax.sharding import PartitionSpec as P

discount = 0.95


def action_table(actions, count):
    return (actions[:, None] == jnp.arange(count, dtype=jnp.int32)[None, :]).astype(jnp.float32)


def picked_rows(indices, hot):
    chosen = jnp.sum(jnp.where(hot[:, :, None] > 0, indices, 0), axis=1)
    return chosen.T


def body(alpha_set, transitions, obs_weights, rewards, chosen_idx, chosen_action):
    actions = rewards.shape[0]
    states = rewards.shape[1]
    obs_local = obs_weights.shape[0]
    bel_rows = chosen_action.shape[0]
    trans_raw = transitions.astype(jnp.float32)
    action_hot = action_table(chosen_action, actions)
    picks = picked_rows(chosen_idx, action_hot).reshape(-1)
    piece = lax.all_gather(alpha_set, "bel", axis=0, tiled=True)
    count = piece.shape[0]
    onehot = (picks[:, None] == jnp.arange(count, dtype=jnp.int32)[None, :]).astype(jnp.bfloat16)
    chosen = jnp.dot(onehot, piece, preferred_element_type=jnp.float32)
    chosen = chosen.reshape(obs_local, bel_rows, states)
    obs_totals, trans_totals = lax.psum(
        (jnp.sum(obs_weights, axis=0), jnp.sum(trans_raw, axis=1)), "obs"
    )
    obs_prob = obs_weights / obs_totals[None, :, :]
    belief_prob = jnp.einsum("ba,oas->obs", action_hot, obs_prob, precision=lax.Precision.HIGHEST)
    partial_value = jnp.sum(belief_prob * chosen, axis=0)
    slice_w = lax.psum_scatter(partial_value, "obs", scatter_dimension=1, tiled=True)
    trans_prob = trans_raw / trans_totals[:, None, :]
    width = slice_w.shape[1]
    spread = (action_hot[:, :, None] * slice_w[:, None, :]).reshape(bel_rows, actions * width)
    table = trans_prob.reshape(actions * width, states)
    owned = bel_rows // lax.axis_size("obs")
    future = lax.psum_scatter(
        jnp.dot(spread, table, precision=lax.Precision.HIGHEST, preferred_element_type=jnp.float32),
        "obs",
        scatter_dimension=0,
        tiled=True,
    )
    own_hot = lax.dynamic_slice_in_dim(action_hot, lax.axis_index("obs") * owned, owned, 0)
    reward_rows = jnp.dot(
        own_hot, rewards, precision=lax.Precision.HIGHEST, preferred_element_type=jnp.float32
    )
    return reward_rows + discount * future


def solution(mesh):
    placed = (
        P("bel", None),
        P(None, "obs", None),
        P("obs", None, None),
        P(),
        P("bel", None, "obs"),
        P("bel"),
    )
    return jax.shard_map(
        body, mesh=mesh, in_specs=placed, out_specs=P(("bel", "obs"), None), check_vma=False
    )
```

profile of v0, /device:TPU:0, one launch (start us, length us, event | category | flops | bytes accessed | tf_op | source)
XLA Modules:
  0.0 457.6 jit_solution(5669605454711230280)
XLA Ops:
  7.4 0.0 copy-start
  7.4 0.0 all-gather.2.cloned.1.call-start
  7.4 0.7 all-gather.2.cloned.1.call-update
  8.1 0.0 all-reduce.3.cloned.1.call-start
  8.1 3.0 reduce_sum.36
  11.2 0.0 copy-start.3
  11.2 0.0 copy-start.1
  11.2 7.7 %convert_reduce_fusion = f32[16,2048]{1,0:T(8,128)} fusion(bf16[16,256,2048]{2,1,0:T(8,128)(2,1)} %param.7), kind=kLoop, calls=%fused_computation.6 | loop fusion | flops 16744448 | bytes 16908288 | tf_op jit(solution)/shard_map/reduce_sum | solution.py:32
  18.9 0.0 all-reduce.3.cloned.1.call-update
  18.9 0.0 reduce-scatter.3.cloned.1.call-start
  19.0 0.0 copy-done.3
  19.0 0.6 iota_compare_fusion.2
  19.6 0.0 copy-done.1
  19.6 0.1 select_reduce_fusion
  19.7 51.1 %all-gather.2.cloned.1.call-done = bf16[2048,2048]{1,0:T(8,128)(2,1)} async-done(((bf16[512,2048]{1,0:T(8,128)(2,1)}), bf16[2048,2048]{1,0:T(8,128)(2,1)}) %all-gather.2.cloned.1.call-update) | async-done | bytes 8388624 | tf_op jit(solution)/shard_map/all_gather | solution.py:26
  70.7 0.0 copy-start.4
  70.8 116.2 %fusion.1 = f32[12288,2048]{1,0:T(8,128)} fusion(bf16[2048,2048]{1,0:T(8,128)(2,1)} %all-gather.2.cloned.1.call-done, s32[12288]{0:T(1024)S(1)} %eq.38), kind=kOutput, calls=%fused_computation.3 | convolution fusion | flops 103104380928 | bytes 109101056 | tf_op jit(solution)/shard_map/dot_general | solution.py:29
  187.0 0.0 all-reduce.3.cloned.1.call-done
  187.0 0.0 copy-done.4
  187.0 0.0 copy-start.2
  187.0 62.6 %fusion = f32[384,2048]{1,0:T(8,128)} fusion(f32[32,384,2048]{2,1,0:T(8,128)} %bitcast.3, f32[32,16,2048]{2,1,0:T(8,128)} %param.8, f32[16,2048]{1,0:T(8,128)} %get-tuple-element.6, s32[384]{0:T(512)S(1)} %copy-done.4), kind=kOutput, calls=%fused_computation.1 | convolution fusion | flops 4882438144 | bytes 108135936 | tf_op jit(solution)/shard_map/ba,oas->obs/dot_general | solution.py:35
  249.6 0.0 copy-start.5
  249.6 0.0 reduce-scatter.3.cloned.1.call-update
  249.6 0.0 reduce-scatter.5.cloned.1.call-start
  249.6 75.1 %reduce-scatter.3.cloned.1.call-done = f32[384,256]{1,0:T(8,128)} async-done(((f32[384,2048]{1,0:T(8,128)}), f32[384,256]{1,0:T(8,128)}) %reduce-scatter.3.cloned.1.call-update) | async-done | bytes 393232 | tf_op jit(solution)/shard_map/reduce_scatter | solution.py:37
  324.8 0.0 copy-done.2
  324.8 1.9 fusion.30
  326.6 0.0 copy-done.5
  326.6 47.3 %fusion.9 = f32[384,2048]{1,0:T(8,128)} fusion(bf16[16,256,2048]{2,1,0:T(8,128)(2,1)} %param.7, f32[16,2048]{1,0:T(8,128)S(1)} %copy-done.5, f32[384,16,256]{2,0,1:T(8,128)S(1)} %fusion.30), kind=kOutput, calls=%fused_computation.13 | convolution fusion | flops 38671482880 | bytes 26345472 | tf_op jit(solution)/shard_map/dot_general | solution.py:44
  373.9 0.0 reduce-scatter.5.cloned.1.call-update
  374.0 73.8 %reduce-scatter.5.cloned.1.call-done = f32[48,2048]{1,0:T(8,128)} async-done(((f32[384,2048]{1,0:T(8,128)}), f32[48,2048]{1,0:T(8,128)}) %reduce-scatter.5.cloned.1.call-update) | async-done | bytes 393232 | tf_op jit(solution)/shard_map/reduce_scatter | solution.py:43
  447.8 0.0 copy-done
  447.8 2.2 convolution_add_fusion
  (1 shorter events, 0.0 us)
Async XLA Ops:
  7.4 440.4 %copy-start = (f32[16,2048]{1,0:T(8,128)S(1)}, f32[16,2048]{1,0:T(8,128)}, u32[]{:S(2)}) copy-start(f32[16,2048]{1,0:T(8,128)} %param.9) | copy-start | bytes 393220
  7.4 63.4 %all-gather.2.cloned.1.call-start = ((), (), s32[]{:S(2)}) async-start(), calls=%async_computation.2 | async-start | bytes 10485760 | tf_op jit(solution)/shard_map/all_gather | solution.py:26
  8.1 178.9 %all-reduce.3.cloned.1.call-start = ((), (), s32[]{:S(2)}) async-start(), calls=%async_computation.5 | async-start | bytes 524288 | tf_op jit(solution)/shard_map/psum | solution.py:31
  11.2 7.8 %copy-start.3 = (s32[384]{0:T(512)S(1)}, s32[384]{0:T(512)}, u32[]{:S(2)}) copy-start(s32[384]{0:T(512)} %param.11) | copy-start | bytes 4612
  11.2 8.4 %copy-start.1 = (s32[384,16,32]{0,2,1:T(8,128)S(1)}, s32[384,16,32]{0,2,1:T(8,128)}, u32[]{:S(2)}) copy-start(s32[384,16,32]{0,2,1:T(8,128)} %param.10) | copy-start | bytes 2359300
  18.9 305.8 %reduce-scatter.3.cloned.1.call-start = ((), (), s32[]{:S(2)}) async-start(), calls=%async_computation.3 | async-start | bytes 3538944 | tf_op jit(solution)/shard_map/reduce_scatter | solution.py:37
  70.7 116.2 %copy-start.4 = (s32[384]{0:T(512)S(1)}, s32[384]{0:T(512)}, u32[]{:S(2)}) copy-start(s32[384]{0:T(512)} %param.11) | copy-start | bytes 4612
  187.0 137.8 %copy-start.2 = (f32[384,16]{0,1:T(8,128)S(1)}, f32[384,16]{0,1:T(8,128)}, u32[]{:S(2)}) copy-start(f32[384,16]{0,1:T(8,128)} %get-tuple-element.9) | copy-start | bytes 73732
  249.6 77.1 %copy-start.5 = (f32[16,2048]{1,0:T(8,128)S(1)}, f32[16,2048]{1,0:T(8,128)}, u32[]{:S(2)}) copy-start(f32[16,2048]{1,0:T(8,128)} %get-tuple-element.5) | copy-start | bytes 393220
  249.6 198.2 %reduce-scatter.5.cloned.1.call-start = ((), (), s32[]{:S(2)}) async-start(), calls=%async_computation.4 | async-start | bytes 3538944 | tf_op jit(solution)/shard_map/reduce_scatter | solution.py:43
Sparse Core Ops, SparseCore 0:
  9.7 60.9 all-gather.1
Sparse Core Ops, SparseCore 1:
  19.0 74.0 all-reduce.2
  249.7 75.0 reduce-scatter.2
  374.1 73.7 reduce-scatter.4
where the time goes:
time: 458 us
  matrix products  228 us (50%)
  waiting for transfers between devices  201 us (44%)
  between operations  15.1 us (3%)
  other arithmetic  13.3 us (3%)
    dot_general x1, matrix products, body(): chosen = jnp.dot(onehot, piece, preferred_element_type=jnp.float32)  116 us
    reduce_scatter x1, waiting for transfers between devices, body(): lax.psum_scatter(partial_value, 'obs', scatter_dimension=1, tiled=True)  75.1 us
    reduce_scatter x1, waiting for transfers between devices, body(): lax.psum_scatter(jnp.dot(spread, table, precision=lax.Precision.HIGHEST,...  73.8 us
    dot_general x1, matrix products, body(): jnp.einsum('ba,oas->obs', action_hot, obs_prob, precision=lax.Precision.H...  62.6 us
    all_gather x1, waiting for transfers between devices, body(): piece = lax.all_gather(alpha_set, 'bel', axis=0, tiled=True)  51.1 us
    dot_general x1, matrix products, body(): jnp.dot(spread, table, precision=lax.Precision.HIGHEST, preferred_element...  47.3 us
  transfers between devices with their start and end apart: 4, of which 3 were waited for; matrix products, arithmetic and copies ran while one was open for 28% of the time, Pallas kernels for 0%

commit v1 on v0

--- a/solution.py
+++ b/solution.py
@@ -4,6 +4,13 @@
 from jax.sharding import PartitionSpec as P
 
 discount = 0.95
+
+
+def supply_all_plate(u, ndim_at):
+    u1 = list(u.shape[1:])
+    u1[ndim_at] *= u.shape[0]
+    low = jnp.moveaxis(u, 0, ndim_at).reshape(u1)
+    return low
 
 
 def action_table(actions, count):
@@ -23,7 +30,29 @@
     trans_raw = transitions.astype(jnp.float32)
     action_hot = action_table(chosen_action, actions)
     picks = picked_rows(chosen_idx, action_hot).reshape(-1)
-    piece = lax.all_gather(alpha_set, "bel", axis=0, tiled=True)
+    workers = lax.axis_size("bel")
+    parts_seen = []
+    for no in range(workers):
+        parts_seen.append((no, (no + 1) % workers))
+    so_far_all = []
+    for ix, c in parts_seen:
+        so_far_all.append((c, ix))
+    all_values, part_next = ([], [])
+    for k0 in range(workers - 1):
+        if k0 % 2 == 0:
+            all_values.append(
+                lax.ppermute(all_values[-1] if all_values else alpha_set, "bel", parts_seen)
+            )
+        else:
+            part_next.append(
+                lax.ppermute(part_next[-1] if part_next else alpha_set, "bel", so_far_all)
+            )
+    formed = jnp.stack([*all_values[::-1], alpha_set, *part_next], 0)
+    seen_now = lax.axis_index("bel")
+    local_part = len(all_values)
+    carry_in = seen_now - local_part
+    formed = formed[(jnp.arange(workers) - carry_in) % workers]
+    piece = supply_all_plate(formed, 0)
     count = piece.shape[0]
     onehot = (picks[:, None] == jnp.arange(count, dtype=jnp.int32)[None, :]).astype(jnp.bfloat16)
     chosen = jnp.dot(onehot, piece, preferred_element_type=jnp.float32)

time: 458 us -> 504 us (1.10)
  waiting for transfers between devices: 201 us -> 217 us
  local copies, waits for them, and re-layouts: 0.03 us -> 14.7 us
  other arithmetic: 13.3 us -> 23.9 us
    all_gather x1 -> x0, waiting for transfers between devices: 51.1 us -> none  [body(): piece = lax.all_gather(alpha_set, 'bel', axis=0, tiled=True)]
    psum x1, waiting for transfers between devices: 0.01 us -> 37.9 us  [body(): lax.psum((jnp.sum(obs_weights, axis=0), jnp.sum(trans_raw, axis=1)), 'obs')]
    ppermute x0 -> x3, waiting for transfers between devices: none -> 32.2 us  [the longest x2 32.2 us: body(): lax.ppermute(all_values[-1] if all_values else alpha_set, 'bel', parts_seen)]
    dot_general x1, matrix products: 116 us -> 133 us  [body(): chosen = jnp.dot(onehot, piece, preferred_element_type=jnp.float32)]
    dot_general x1, matrix products: 62.6 us -> 47.1 us  [body(): jnp.einsum('ba,oas->obs', action_hot, obs_prob, precision=lax.Precision.H...]
    gather x0 -> x3, local copies, waits for them, and re-layouts: none -> 13.5 us  [body(): formed = formed[(jnp.arange(workers) - carry_in) % workers]]
    unnamed x0 -> x1, other arithmetic: none -> 8.24 us
    ppermute x0 -> x3, starting transfers between devices: none -> 5.06 us  [the longest x2 3.12 us: body(): lax.ppermute(all_values[-1] if all_values else alpha_set, 'bel', parts_seen)]
  transfers between devices with their start and end apart: 4 -> 6, of which waited for: 3 -> 4; matrix products, arithmetic and copies ran while one was open for 28% -> 12% of each run, Pallas kernels for 0% -> 0%
where the time goes in v1:
time: 504 us
  matrix products  229 us (45%)
  waiting for transfers between devices  217 us (43%)
  other arithmetic  23.9 us (5%)
  local copies, waits for them, and re-layouts  14.7 us (3%)
  between operations  13.2 us (3%)
  starting transfers between devices  5.14 us (1%)
    dot_general x1, matrix products, body(): chosen = jnp.dot(onehot, piece, preferred_element_type=jnp.float32)  133 us
    reduce_scatter x1, waiting for transfers between devices, body(): lax.psum_scatter(partial_value, 'obs', scatter_dimension=1, tiled=True)  73.7 us
    reduce_scatter x1, waiting for transfers between devices, body(): lax.psum_scatter(jnp.dot(spread, table, precision=lax.Precision.HIGHEST,...  73.5 us
    dot_general x1, matrix products, body(): jnp.dot(spread, table, precision=lax.Precision.HIGHEST, preferred_element...  47.3 us
    dot_general x1, matrix products, body(): jnp.einsum('ba,oas->obs', action_hot, obs_prob, precision=lax.Precision.H...  47.1 us
    psum x1, waiting for transfers between devices, body(): lax.psum((jnp.sum(obs_weights, axis=0), jnp.sum(trans_raw, axis=1)), 'obs')  37.9 us
    ppermute x2, waiting for transfers between devices, body(): lax.ppermute(all_values[-1] if all_values else alpha_set, 'bel', parts_seen)  32.2 us
    gather x3, local copies, waits for them, and re-layouts, body(): formed = formed[(jnp.arange(workers) - carry_in) % workers]  13.5 us
  transfers between devices with their start and end apart: 6, of which 4 were waited for; matrix products, arithmetic and copies ran while one was open for 12% of the time, Pallas kernels for 0%

profile of v1, /device:TPU:0, one launch (start us, length us, event | category | flops | bytes accessed | tf_op | source)
XLA Modules:
  0.0 503.6 jit_solution(16297428703179448242)
XLA Ops:
  6.5 0.0 copy-start
  6.5 0.0 all-reduce.3.cloned.1.call-start
  6.5 0.5 collective-permute-start
  7.0 1.9 collective-permute-start.2
  9.0 3.0 reduce_sum.36
  12.0 0.0 copy-start.4
  12.0 0.0 copy-start.2
  12.0 7.7 %convert_reduce_fusion = f32[16,2048]{1,0:T(8,128)} fusion(bf16[16,256,2048]{2,1,0:T(8,128)(2,1)} %param.7), kind=kLoop, calls=%fused_computation.9 | loop fusion | flops 16744448 | bytes 16908288 | tf_op jit(solution)/shard_map/reduce_sum | solution.py:61
  19.7 0.0 all-reduce.3.cloned.1.call-update
  19.8 0.0 reduce-scatter.3.cloned.1.call-start
  19.8 0.0 copy-done.4
  19.8 0.6 iota_compare_fusion.1
  20.5 0.0 copy-done.2
  20.5 0.1 select_reduce_fusion
  20.6 32.2 %collective-permute-done = bf16[512,2048]{1,0:T(8,128)(2,1)S(1)} collective-permute-done((bf16[512,2048]{1,0:T(8,128)(2,1)}, bf16[512,2048]{1,0:T(8,128)(2,1)S(1)}, u32[]{:S(2)}, u32[]{:S(2)}) %collective-permute-start) | collective-permute-done | bytes 2097184 | tf_op jit(solution)/shard_map/ppermute | solution.py:44
  52.8 2.6 collective-permute-start.1
  55.4 37.9 %all-reduce.3.cloned.1.call-done = (f32[16,2048]{1,0:T(8,128)}, f32[16,2048]{1,0:T(8,128)}) async-done(((f32[16,2048]{1,0:T(8,128)}, f32[16,2048]{1,0:T(8,128)}), (f32[16,2048]{1,0:T(8,128)}, f32[16,2048]{1,0:T(8,128)})) %all-reduce.3.cloned.1.call-update) | async-done | bytes 262160 | tf_op jit(solution)/shard_map/psum | solution.py:60
  93.3 0.0 copy-start.1
  93.3 47.1 %fusion.10 = f32[32,2048,384]{2,1,0:T(8,128)} fusion(f32[32,16,2048]{2,1,0:T(8,128)} %param.8, f32[16,2048]{1,0:T(8,128)} %get-tuple-element.6, s32[384]{0:T(512)S(1)} %copy-done.4), kind=kOutput, calls=%fused_computation.15 | convolution fusion | flops 4832892928 | bytes 104990208 | tf_op jit(solution)/shard_map/ba,oas->obs/dot_general | solution.py:64
  140.4 0.0 collective-permute-done.2
  140.4 0.0 collective-permute-done.1
  140.4 0.0 copy-done.1
  140.4 3.3 pad_maximum_fusion
  143.7 3.7 fusion.25
  147.4 4.9 gather_fusion
  152.4 4.9 gather_fusion.1
  157.3 8.2 %pad_maximum_fusion.1 = bf16[4,512,2048]{2,1,0:T(8,128)(2,1)} fusion(bf16[4,512,1024]{2,1,0:T(8,128)(2,1)} %gather_fusion.1, bf16[4,512,1024]{2,1,0:T(8,128)(2,1)} %gather_fusion), kind=kLoop, calls=%fused_computation.13 | loop fusion | flops 16777216 | bytes 16777216
  165.5 0.0 copy-start.3
  165.5 132.7 %fusion = f32[384,2048]{0,1:T(8,128)} fusion(f32[32,2048,384]{2,1,0:T(8,128)} %fusion.10, bf16[2048,2048,1]{1,0,2:T(8,128)(2,1)} %bitcast.36, s32[32,384]{1,0:T(8,128)S(1)} %bitcast.39), kind=kOutput, calls=%fused_computation.3 | convolution fusion | flops 103153926144 | bytes 112246784 | tf_op jit(solution)/shard_map/dot_general | solution.py:58
  298.3 0.0 copy-start.5
  298.3 0.0 reduce-scatter.3.cloned.1.call-update
  298.3 0.0 reduce-scatter.5.cloned.1.call-start
  298.4 73.7 %reduce-scatter.3.cloned.1.call-done = f32[384,256]{0,1:T(8,128)} async-done(((f32[384,2048]{0,1:T(8,128)}), f32[384,256]{0,1:T(8,128)}) %reduce-scatter.3.cloned.1.call-update) | async-done | bytes 393232 | tf_op jit(solution)/shard_map/reduce_scatter | solution.py:66
  372.0 1.2 copy.9
  373.2 0.0 copy-done.3
  373.2 0.9 fusion.40
  374.1 0.0 copy-done.5
  374.1 47.3 %fusion.14 = f32[384,2048]{1,0:T(8,128)} fusion(bf16[16,256,2048]{2,1,0:T(8,128)(2,1)} %param.7, f32[16,2048]{1,0:T(8,128)S(1)} %copy-done.5, f32[384,16,256]{2,0,1:T(8,128)S(1)} %fusion.40), kind=kOutput, calls=%fused_computation.19 | convolution fusion | flops 38671482880 | bytes 26345472 | tf_op jit(solution)/shard_map/dot_general | solution.py:73
  421.4 0.0 reduce-scatter.5.cloned.1.call-update
  421.4 73.5 %reduce-scatter.5.cloned.1.call-done = f32[48,2048]{1,0:T(8,128)} async-done(((f32[384,2048]{1,0:T(8,128)}), f32[48,2048]{1,0:T(8,128)}) %reduce-scatter.5.cloned.1.call-update) | async-done | bytes 393232 | tf_op jit(solution)/shard_map/reduce_scatter | solution.py:72
  494.9 0.0 copy-done
  494.9 2.2 convolution_add_fusion
  (2 shorter events, 0.0 us)
Async XLA Ops:
  6.5 488.4 %copy-start = (f32[16,2048]{1,0:T(8,128)S(1)}, f32[16,2048]{1,0:T(8,128)}, u32[]{:S(2)}) copy-start(f32[16,2048]{1,0:T(8,128)} %param.9) | copy-start | bytes 393220
  6.5 86.8 %all-reduce.3.cloned.1.call-start = ((), (), s32[]{:S(2)}) async-start(), calls=%async_computation.4 | async-start | bytes 524288 | tf_op jit(solution)/shard_map/psum | solution.py:60
  6.5 46.2 %collective-permute-start = (bf16[512,2048]{1,0:T(8,128)(2,1)}, bf16[512,2048]{1,0:T(8,128)(2,1)S(1)}, u32[]{:S(2)}, u32[]{:S(2)}) collective-permute-start(bf16[512,2048]{1,0:T(8,128)(2,1)} %param.6), channel_id=1, source_target_pairs={{0,1},{1,2},{2,3},{3,0},{4,5},{5,6},{6,7},{7,4},{8,9},{9,10},{10,1... | collective-permute-start | bytes 6291464 | tf_op jit(solution)/shard_map/ppermute | solution.py:44
  7.0 133.3 %collective-permute-start.2 = (bf16[512,2048]{1,0:T(8,128)(2,1)}, bf16[512,2048]{1,0:T(8,128)(2,1)}, u32[]{:S(2)}, u32[]{:S(2)}) collective-permute-start(bf16[512,2048]{1,0:T(8,128)(2,1)} %param.6), channel_id=1, source_target_pairs={{1,0},{2,1},{3,2},{0,3},{5,4},{6,5},{7,6},{4,7},{9,8},{10,9},{11,1... | collective-permute-start | bytes 6291464 | tf_op jit(solution)/shard_map/ppermute | solution.py:48
  12.0 7.8 %copy-start.4 = (s32[384]{0:T(512)S(1)}, s32[384]{0:T(512)}, u32[]{:S(2)}) copy-start(s32[384]{0:T(512)} %param.11) | copy-start | bytes 4612
  12.0 8.4 %copy-start.2 = (s32[384,16,32]{0,2,1:T(8,128)S(1)}, s32[384,16,32]{0,2,1:T(8,128)}, u32[]{:S(2)}) copy-start(s32[384,16,32]{0,2,1:T(8,128)} %param.10) | copy-start | bytes 2359300
  19.8 352.3 %reduce-scatter.3.cloned.1.call-start = ((), (), s32[]{:S(2)}) async-start(), calls=%async_computation.2 | async-start | bytes 3538944 | tf_op jit(solution)/shard_map/reduce_scatter | solution.py:66
  52.8 87.6 %collective-permute-start.1 = (bf16[512,2048]{1,0:T(8,128)(2,1)S(1)}, bf16[512,2048]{1,0:T(8,128)(2,1)}, u32[]{:S(2)}, u32[]{:S(2)}) collective-permute-start(bf16[512,2048]{1,0:T(8,128)(2,1)S(1)} %collective-permute-done), channel_id=1, source_target_pairs={{0,1},{1,2},{2,3},{3,0},{4,5},{5,6},{6,7},{7,4},{8,9},{9,10},{10,1... | collective-permute-start | bytes 6291464 | tf_op jit(solution)/shard_map/ppermute | solution.py:44
  93.3 47.1 %copy-start.1 = (bf16[512,2048]{1,0:T(8,128)(2,1)S(1)}, bf16[512,2048]{1,0:T(8,128)(2,1)}, u32[]{:S(2)}) copy-start(bf16[512,2048]{1,0:T(8,128)(2,1)} %param.6) | copy-start | bytes 6291460
  165.5 207.7 %copy-start.3 = (f32[384,16]{0,1:T(8,128)S(1)}, f32[384,16]{0,1:T(8,128)}, u32[]{:S(2)}) copy-start(f32[384,16]{0,1:T(8,128)} %get-tuple-element.11) | copy-start | bytes 73732
  298.3 75.8 %copy-start.5 = (f32[16,2048]{1,0:T(8,128)S(1)}, f32[16,2048]{1,0:T(8,128)}, u32[]{:S(2)}) copy-start(f32[16,2048]{1,0:T(8,128)} %get-tuple-element.5) | copy-start | bytes 393220
  298.3 196.6 %reduce-scatter.5.cloned.1.call-start = ((), (), s32[]{:S(2)}) async-start(), calls=%async_computation.3 | async-start | bytes 3538944 | tf_op jit(solution)/shard_map/reduce_scatter | solution.py:72
Sparse Core Ops, SparseCore 0:
  19.9 73.3 all-reduce.2
  298.4 73.5 reduce-scatter.2
  421.6 73.2 reduce-scatter.4
